TPU v7x, 32 devices: a whole 2x2x4 slice. The times are simulated.
32 devices in a mesh: layer: 4 (over y, x), latent: 8 (over z, core).
Axes of the slice: x: 2, y: 2, z: 4, core: 2. Of those that a mesh axis runs over, the one named last changes fastest.
Arguments:
- tokens: bfloat16 [128, 16384], P('latent', 'layer'), may hold values from -6 to 6
- encoder_weight: bfloat16 [16384, 16384], P('layer', 'latent'), may hold values from -0.046875 to 0.046875
- encoder_bias: float32 [16384], P('latent'), may hold values from -3 to 3, as said below
- decoder_weight: bfloat16 [16384, 16384], P('latent', 'layer'), may hold values from -2 to 2
- decoder_bias: float32 [16384], P('layer'), may hold values from -12 to 12
Outputs:
- encoder_grad: bfloat16 [16384, 16384], P('layer', 'latent')
- decoder_grad: bfloat16 [16384, 16384], P('latent', 'layer')
Inputs may be any that keep to these rules, and one draw needn't show every extreme that they name: `encoder_bias`: mean about -0.5.
All inputs are finite; a program needn't handle non-finite values.
Results may differ from a plain program's by a relative error of at most 0.0059.
Values may be sent and summed in bfloat16 or wider, within the bound.
No kernel may reach another device: no remote copies, remote signals or barrier semaphores. Data moves between devices by JAX's collectives and lax.ppermute only.
A program may use at most 128 MiB of HBM per device.

v0:
```python
import jax
import jax.numpy as jnp
from jax import lax
from jax.sharding import PartitionSpec as P

L = 4
D = 4096
LOSS_SCALE = 0.0625
SPARSITY = 0.5
sharpness = 4.0
epsilon = 1e-06


def shards(tokens, encoder_weight, encoder_bias, decoder_weight, decoder_bias):
    rows_dev, width_dev = tokens.shape
    latents_dev = encoder_weight.shape[1]
    groups = lax.axis_size("layer")
    layer_index = lax.axis_index("layer") * width_dev // D
    wide = decoder_weight.astype(jnp.float32)
    squares_own = jnp.sum(wide * wide, axis=1)
    placed = jnp.where(jnp.arange(L)[:, None] == layer_index, squares_own[None, :], 0.0)
    squares = lax.psum(placed, "layer")
    row_norms = jnp.sqrt(squares + epsilon)
    weights_sum = jnp.sum(row_norms, axis=0)
    own_norm = lax.dynamic_slice_in_dim(row_norms, layer_index, 1, 0)[0]
    every_token = lax.all_gather(tokens, "latent", axis=0, tiled=True)
    partial_value = jnp.dot(every_token, encoder_weight, preferred_element_type=jnp.float32)
    share_width = latents_dev // groups
    offset = lax.axis_index("layer") * share_width
    preact = lax.psum_scatter(partial_value, "layer", scatter_dimension=1, tiled=True)
    preact = preact + lax.dynamic_slice_in_dim(encoder_bias, offset, share_width, 0)[None, :]
    hidden_share = (jax.nn.softplus(sharpness * preact) / sharpness).astype(jnp.bfloat16)
    hidden = lax.all_gather(hidden_share, "layer", axis=1, tiled=True)
    slopes = jax.nn.sigmoid(sharpness * preact)
    rebuilt = lax.psum(
        jnp.dot(hidden, decoder_weight, preferred_element_type=jnp.float32), "latent"
    )
    errors = rebuilt + decoder_bias[None, :] - every_token.astype(jnp.float32)
    error_grad = (LOSS_SCALE * errors).astype(jnp.bfloat16)
    back_terms = lax.dot_general(
        error_grad, decoder_weight, (((1,), (1,)), ((), ())), preferred_element_type=jnp.float32
    )
    summed = lax.psum_scatter(back_terms, "layer", scatter_dimension=1, tiled=True)
    penalty = lax.dynamic_slice_in_dim(weights_sum, offset, share_width, 0)
    grad_share = ((summed + LOSS_SCALE * SPARSITY * penalty[None, :]) * slopes).astype(jnp.bfloat16)
    pre_grad = lax.all_gather(grad_share, "layer", axis=1, tiled=True)
    encoder_grad = lax.dot_general(
        every_token, pre_grad, (((0,), (0,)), ((), ())), preferred_element_type=jnp.float32
    ).astype(jnp.bfloat16)
    totals = jnp.sum(hidden.astype(jnp.float32), axis=0)
    direct = lax.dot_general(
        hidden, error_grad, (((0,), (0,)), ((), ())), preferred_element_type=jnp.float32
    )
    sparse_term = wide * (LOSS_SCALE * SPARSITY * totals / own_norm)[:, None]
    decoder_grad = (direct + sparse_term).astype(jnp.bfloat16)
    return (encoder_grad, decoder_grad)


def solution(mesh):
    placed = (
        P("latent", "layer"),
        P("layer", "latent"),
        P("latent"),
        P("latent", "layer"),
        P("layer"),
    )
    return jax.shard_map(
        shards,
        mesh=mesh,
        in_specs=placed,
        out_specs=(P("layer", "latent"), P("latent", "layer")),
        check_vma=False,
    )
```

profile of v0, /device:TPU:0, one launch (start us, length us, event | category | flops | bytes accessed | tf_op | source)
XLA Modules:
  0.0 247.9 jit_solution(9035878231300968238)
XLA Ops:
  7.2 0.0 all-gather.2.cloned.1.call-start
  7.2 0.7 all-gather.2.cloned.1.call-update
  7.9 0.0 reduce-scatter.3.cloned.1.call-start
  7.9 26.6 %all-gather.2.cloned.1.call-done = bf16[128,4096]{1,0:T(8,128)(2,1)} async-done(((bf16[16,4096]{1,0:T(8,128)(2,1)}), bf16[128,4096]{1,0:T(8,128)(2,1)}) %all-gather.2.cloned.1.call-update) | async-done | bytes 1048592 | tf_op jit(solution)/shard_map/all_gather | solution.py:26
  34.6 9.4 %fusion.6 = f32[128,2048]{1,0:T(8,128)} fusion(bf16[128,4096]{1,0:T(8,128)(2,1)} %all-gather.2.cloned.1.call-done, bf16[4096,2048]{1,0:T(8,128)(2,1)} %param.6), kind=kOutput, calls=%fused_computation.20 | convolution fusion | flops 2147483648 | bytes 18874368 | tf_op jit(solution)/shard_map/dot_general | solution.py:27
  44.0 0.0 reduce-scatter.3.cloned.1.call-update
  44.0 0.0 all-reduce.2.cloned.1.call-start
  44.1 0.8 dynamic_slice.9
  44.8 26.9 %reduce-scatter.3.cloned.1.call-done = f32[128,512]{1,0:T(8,128)} async-done(((f32[128,2048]{1,0:T(8,128)}), f32[128,512]{1,0:T(8,128)}) %reduce-scatter.3.cloned.1.call-update) | async-done | bytes 262160 | tf_op jit(solution)/shard_map/reduce_scatter | solution.py:30
  71.7 1.1 fusion.4
  72.8 10.1 %all_gather.10 = bf16[128,2048]{1,0:T(8,128)(2,1)S(1)} all-gather(bf16[128,512]{1,0:T(8,128)(2,1)S(1)} %fusion.4), channel_id=1, replica_groups=mesh['layer'=4,'latent'=8] {'layer'}, dimensions={1}, use_global_device_ids=true | all-gather | bytes 655360 | tf_op jit(solution)/shard_map/all_gather | solution.py:33
  82.9 0.0 copy-start
  82.9 0.0 copy-start.2
  82.9 9.5 %fusion.7 = f32[128,4096]{1,0:T(8,128)} fusion(bf16[128,2048]{1,0:T(8,128)(2,1)S(1)} %all_gather.10, bf16[2048,4096]{1,0:T(8,128)(2,1)} %param.8), kind=kOutput, calls=%fused_computation.21 | convolution fusion | flops 2147483648 | bytes 19398656 | tf_op jit(solution)/shard_map/dot_general | solution.py:36
  92.4 0.0 all-reduce.2.cloned.1.call-update
  92.5 0.0 reduce-scatter.5.cloned.1.call-start
  92.5 7.4 %fusion = f32[2048]{0:T(1024)S(1)} fusion(bf16[2048,4096]{1,0:T(8,128)(2,1)} %param.8), kind=kLoop, calls=%fused_computation.2 | loop fusion | flops 25163776 | bytes 16785408 | tf_op jit(solution)/shard_map/reduce_sum | solution.py:20
  99.9 0.1 broadcast_select_fusion
  100.0 15.1 %psum.15 = f32[4,2048]{1,0:T(4,128)S(1)} all-reduce(f32[4,2048]{1,0:T(4,128)S(1)} %broadcast_select_fusion), channel_id=1, replica_groups=mesh['layer'=4,'latent'=8] {'layer'}, use_global_device_ids=true, to_apply=%region_4.5 | all-reduce | flops 8192 | bytes 65536 | tf_op jit(solution)/shard_map/psum | solution.py:22
  115.2 42.5 %all-reduce.2.cloned.1.call-done = f32[128,4096]{1,0:T(8,128)} async-done(((f32[128,4096]{1,0:T(8,128)}), f32[128,4096]{1,0:T(8,128)}) %all-reduce.2.cloned.1.call-update) | async-done | bytes 2097168 | tf_op jit(solution)/shard_map/psum | solution.py:35
  157.7 0.0 copy-done
  157.7 0.0 copy-done.2
  157.7 1.9 multiply_convert_fusion
  159.6 12.4 %fusion.8 = f32[128,2048]{1,0:T(8,128)} fusion(bf16[128,4096]{1,0:T(8,128)(2,1)S(1)} %multiply_convert_fusion, bf16[2048,4096]{1,0:T(8,128)(2,1)} %param.8), kind=kOutput, calls=%fused_computation.22 | convolution fusion | flops 2147483648 | bytes 18874368 | tf_op jit(solution)/shard_map/dot_general | solution.py:40
  172.0 0.0 reduce-scatter.5.cloned.1.call-update
  172.0 0.1 dynamic-slice_multiply_fusion
  172.1 0.1 convert_reduce_fusion
  172.2 0.0 copy-start.1
  172.2 12.0 %fusion.2 = bf16[2048,4096]{1,0:T(8,128)(2,1)} fusion(bf16[2048,4096]{1,0:T(8,128)(2,1)} %param.8, f32[2048]{0:T(1024)S(1)} %multiply_divide_fusion, bf16[128,2048]{1,0:T(8,128)(2,1)S(1)} %all_gather.10, bf16[128,4096]{1,0:T(8,128)(2,1)S(1)} %multiply_convert_fusion), kind=kOutput, calls=%fused_computation.4 | convolution fusion | flops 2181038080 | bytes 35135488 | tf_op jit(solution)/shard_map/dot_general | solution.py:51
  184.2 15.5 %reduce-scatter.5.cloned.1.call-done = f32[128,512]{1,0:T(8,128)} async-done(((f32[128,2048]{1,0:T(8,128)}), f32[128,512]{1,0:T(8,128)}) %reduce-scatter.5.cloned.1.call-update) | async-done | bytes 262160 | tf_op jit(solution)/shard_map/reduce_scatter | solution.py:43
  199.7 0.0 copy-done.1
  199.7 1.0 multiply_convert_fusion.1
  200.8 10.1 %all_gather.11 = bf16[128,2048]{1,0:T(8,128)(2,1)S(1)} all-gather(bf16[128,512]{1,0:T(8,128)(2,1)S(1)} %multiply_convert_fusion.1), channel_id=1, replica_groups=mesh['layer'=4,'latent'=8] {'layer'}, dimensions={1}, use_global_device_ids=true | all-gather | bytes 655360 | tf_op jit(solution)/shard_map/all_gather | solution.py:46
  210.8 8.1 %convert_bitcast_fusion = bf16[4096,2048]{0,1:T(8,128)(2,1)} fusion(bf16[128,2048]{1,0:T(8,128)(2,1)S(1)} %all_gather.11, bf16[128,4096]{1,0:T(8,128)(2,1)S(1)} %copy-done), kind=kOutput, calls=%fused_computation.5 | convolution fusion | flops 2155872256 | bytes 18350080 | tf_op jit(solution)/shard_map/dot_general | solution.py:47
  218.9 22.4 %copy.8 = bf16[4096,2048]{1,0:T(8,128)(2,1)} copy(bf16[4096,2048]{0,1:T(8,128)(2,1)} %convert_bitcast_fusion) | data formatting | bytes 33554432
  (4 shorter events, 0.1 us)
Async XLA Ops:
  7.2 27.4 %all-gather.2.cloned.1.call-start = ((), (), s32[]{:S(2)}) async-start(), calls=%async_computation.2 | async-start | bytes 1179648 | tf_op jit(solution)/shard_map/all_gather | solution.py:26
  7.9 63.8 %reduce-scatter.3.cloned.1.call-start = ((), (), s32[]{:S(2)}) async-start(), calls=%async_computation.3 | async-start | bytes 1310720 | tf_op jit(solution)/shard_map/reduce_scatter | solution.py:30
  44.0 113.7 %all-reduce.2.cloned.1.call-start = ((), (), s32[]{:S(2)}) async-start(), calls=%async_computation.4 | async-start | bytes 4194304 | tf_op jit(solution)/shard_map/psum | solution.py:35
  82.9 74.8 %copy-start = (bf16[128,4096]{1,0:T(8,128)(2,1)S(1)}, bf16[128,4096]{1,0:T(8,128)(2,1)}, u32[]{:S(2)}) copy-start(bf16[128,4096]{1,0:T(8,128)(2,1)} %all-gather.2.cloned.1.call-done) | copy-start | bytes 3145732
  82.9 74.8 %copy-start.2 = (f32[4096]{0:T(1024)S(1)}, f32[4096]{0:T(1024)}, u32[]{:S(2)}) copy-start(f32[4096]{0:T(1024)} %param.9) | copy-start | bytes 49156
  92.5 107.3 %reduce-scatter.5.cloned.1.call-start = ((), (), s32[]{:S(2)}) async-start(), calls=%async_computation.5 | async-start | bytes 1310720 | tf_op jit(solution)/shard_map/reduce_scatter | solution.py:43
  172.2 27.5 %copy-start.1 = (f32[128,512]{1,0:T(8,128)S(1)}, f32[128,512]{1,0:T(8,128)}, u32[]{:S(2)}) copy-start(f32[128,512]{1,0:T(8,128)} %reduce-scatter.3.cloned.1.call-done) | copy-start | bytes 786436
Sparse Core Ops, SparseCore 0:
  9.6 24.9 all-gather.1
  44.1 27.5 reduce-scatter.2
  92.6 65.0 all-reduce.1
  172.1 27.5 reduce-scatter.4
where the time goes:
time: 249 us; the launch traced here: 248 us
  waiting for transfers between devices  112 us (45%)
  matrix products  51.3 us (21%)
  blocking collectives  35.3 us (14%)
  local copies, waits for them, and re-layouts  23.2 us (9%)
  between operations  13.9 us (6%)
  other arithmetic  11.7 us (5%)
    psum x1, waiting for transfers between devices, shards(): lax.psum(jnp.dot(hidden, decoder_weight, preferred_element_type=jnp.float...  42.5 us
    reduce_scatter x1, waiting for transfers between devices, shards(): lax.psum_scatter(partial_value, 'layer', scatter_dimension=1, tiled=True)  26.9 us
    all_gather x1, waiting for transfers between devices, shards(): every_token = lax.all_gather(tokens, 'latent', axis=0, tiled=True)  26.6 us
    unnamed x7, local copies, waits for them, and re-layouts  22.4 us
    reduce_scatter x1, waiting for transfers between devices, shards(): lax.psum_scatter(back_terms, 'layer', scatter_dimension=1, tiled=True)  15.5 us
    psum x1, blocking collectives, shards(): squares = lax.psum(placed, 'layer')  15.1 us
    dot_general x1, matrix products, shards(): lax.dot_general(error_grad, decoder_weight, (((1,), (1,)), ((), ())), pre...  12.4 us
    dot_general x1, matrix products, shards(): lax.dot_general(hidden, error_grad, (((0,), (0,)), ((), ())), preferred_e...  12 us
  transfers between devices with their start and end apart: 4, of which 4 were waited for; matrix products, arithmetic and copies ran while one was open for 8% of the time, Pallas kernels for 0%

commit v1 on v0

--- a/solution.py
+++ b/solution.py
@@ -32,8 +32,11 @@
     hidden_share = (jax.nn.softplus(sharpness * preact) / sharpness).astype(jnp.bfloat16)
     hidden = lax.all_gather(hidden_share, "layer", axis=1, tiled=True)
     slopes = jax.nn.sigmoid(sharpness * preact)
-    rebuilt = lax.psum(
-        jnp.dot(hidden, decoder_weight, preferred_element_type=jnp.float32), "latent"
+    rebuilt = jnp.sum(
+        lax.all_gather(
+            jnp.dot(hidden, decoder_weight, preferred_element_type=jnp.float32), "latent"
+        ),
+        axis=0,
     )
     errors = rebuilt + decoder_bias[None, :] - every_token.astype(jnp.float32)
     error_grad = (LOSS_SCALE * errors).astype(jnp.bfloat16)

time: 249 us -> 342 us (1.37)
  waiting for transfers between devices: 112 us -> 197 us
  other arithmetic: 11.7 us -> 20.4 us
    all_gather x0 -> x1, waiting for transfers between devices: none -> 128 us  [shards(): lax.all_gather(jnp.dot(hidden, decoder_weight, preferred_element_type=jnp...]
    psum x1 -> x0, waiting for transfers between devices: 42.5 us -> none  [shards(): lax.psum(jnp.dot(hidden, decoder_weight, preferred_element_type=jnp.float...]
    reduce_sum x0 -> x1, other arithmetic: none -> 8.68 us  [shards(): jnp.sum(lax.all_gather(jnp.dot(hidden, decoder_weight, preferred_element_...]
  transfers between devices with their start and end apart: 4 -> 4, of which waited for: 4 -> 4; matrix products, arithmetic and copies ran while one was open for 8% -> 6% of each run, Pallas kernels for 0% -> 0%
where the time goes in v1:
time: 342 us; the launch traced here: 341 us
  waiting for transfers between devices  197 us (58%)
  matrix products  51.3 us (15%)
  blocking collectives  35.4 us (10%)
  local copies, waits for them, and re-layouts  23.2 us (7%)
  other arithmetic  20.4 us (6%)
  between operations  13.9 us (4%)
    all_gather x1, waiting for transfers between devices, shards(): lax.all_gather(jnp.dot(hidden, decoder_weight, preferred_element_type=jnp...  128 us
    reduce_scatter x1, waiting for transfers between devices, shards(): lax.psum_scatter(partial_value, 'layer', scatter_dimension=1, tiled=True)  26.9 us
    all_gather x1, waiting for transfers between devices, shards(): every_token = lax.all_gather(tokens, 'latent', axis=0, tiled=True)  26.6 us
    unnamed x7, local copies, waits for them, and re-layouts  22.4 us
    psum x1, blocking collectives, shards(): squares = lax.psum(placed, 'layer')  15.2 us
    reduce_scatter x1, waiting for transfers between devices, shards(): lax.psum_scatter(back_terms, 'layer', scatter_dimension=1, tiled=True)  14.1 us
    dot_general x1, matrix products, shards(): lax.dot_general(error_grad, decoder_weight, (((1,), (1,)), ((), ())), pre...  12.4 us
    dot_general x1, matrix products, shards(): lax.dot_general(hidden, error_grad, (((0,), (0,)), ((), ())), preferred_e...  12 us
  transfers between devices with their start and end apart: 4, of which 4 were waited for; matrix products, arithmetic and copies ran while one was open for 6% of the time, Pallas kernels for 0%

profile of v1, /device:TPU:0, one launch (start us, length us, event | category | flops | bytes accessed | tf_op | source)
XLA Modules:
  0.0 341.0 jit_solution(1450849716740138458)
XLA Ops:
  7.2 0.0 all-gather.4.cloned.1.call-start
  7.2 0.7 all-gather.4.cloned.1.call-update
  7.9 0.0 reduce-scatter.3.cloned.1.call-start
  7.9 26.6 %all-gather.4.cloned.1.call-done = bf16[128,4096]{1,0:T(8,128)(2,1)} async-done(((bf16[16,4096]{1,0:T(8,128)(2,1)}), bf16[128,4096]{1,0:T(8,128)(2,1)}) %all-gather.4.cloned.1.call-update) | async-done | bytes 1048592 | tf_op jit(solution)/shard_map/all_gather | solution.py:26
  34.6 9.4 %fusion.6 = f32[128,2048]{1,0:T(8,128)} fusion(bf16[128,4096]{1,0:T(8,128)(2,1)} %all-gather.4.cloned.1.call-done, bf16[4096,2048]{1,0:T(8,128)(2,1)} %param.6), kind=kOutput, calls=%fused_computation.20 | convolution fusion | flops 2147483648 | bytes 18874368 | tf_op jit(solution)/shard_map/dot_general | solution.py:27
  44.0 0.0 reduce-scatter.3.cloned.1.call-update
  44.0 0.0 all-gather.6.cloned.1.call-start
  44.1 0.8 dynamic_slice.9
  44.8 26.9 %reduce-scatter.3.cloned.1.call-done = f32[128,512]{1,0:T(8,128)} async-done(((f32[128,2048]{1,0:T(8,128)}), f32[128,512]{1,0:T(8,128)}) %reduce-scatter.3.cloned.1.call-update) | async-done | bytes 262160 | tf_op jit(solution)/shard_map/reduce_scatter | solution.py:30
  71.7 1.1 fusion.4
  72.8 10.1 %all_gather.16 = bf16[128,2048]{1,0:T(8,128)(2,1)S(1)} all-gather(bf16[128,512]{1,0:T(8,128)(2,1)S(1)} %fusion.4), channel_id=1, replica_groups=mesh['layer'=4,'latent'=8] {'layer'}, dimensions={1}, use_global_device_ids=true | all-gather | bytes 655360 | tf_op jit(solution)/shard_map/all_gather | solution.py:33
  82.9 9.4 %fusion.7 = f32[128,4096]{1,0:T(8,128)} fusion(bf16[128,2048]{1,0:T(8,128)(2,1)S(1)} %all_gather.16, bf16[2048,4096]{1,0:T(8,128)(2,1)} %param.8), kind=kOutput, calls=%fused_computation.21 | convolution fusion | flops 2147483648 | bytes 19398656 | tf_op jit(solution)/shard_map/dot_general | solution.py:37
  92.3 0.0 all-gather.6.cloned.1.call-update
  92.4 0.0 reduce-scatter.5.cloned.1.call-start
  92.4 0.0 copy-start
  92.4 0.0 copy-start.2
  92.5 7.4 %fusion = f32[2048]{0:T(1024)S(1)} fusion(bf16[2048,4096]{1,0:T(8,128)(2,1)} %param.8), kind=kLoop, calls=%fused_computation.2 | loop fusion | flops 25163776 | bytes 16785408 | tf_op jit(solution)/shard_map/reduce_sum | solution.py:20
  99.9 0.1 broadcast_select_fusion
  99.9 15.2 %psum.7 = f32[4,2048]{1,0:T(4,128)S(1)} all-reduce(f32[4,2048]{1,0:T(4,128)S(1)} %broadcast_select_fusion), channel_id=1, replica_groups=mesh['layer'=4,'latent'=8] {'layer'}, use_global_device_ids=true, to_apply=%region_4.5 | all-reduce | flops 8192 | bytes 65536 | tf_op jit(solution)/shard_map/psum | solution.py:22
  115.2 128.4 %all-gather.6.cloned.1.call-done = f32[1024,4096]{1,0:T(8,128)} async-done(((f32[128,4096]{1,0:T(8,128)}), f32[1024,4096]{1,0:T(8,128)}) %all-gather.6.cloned.1.call-update) | async-done | bytes 16777232 | tf_op jit(solution)/shard_map/all_gather | solution.py:36
  243.6 8.7 %reduce_sum.36 = f32[128,4096]{1,0:T(8,128)} reduce(f32[8,128,4096]{2,1,0:T(8,128)} %bitcast.14, f32[]{:T(128)} %constant.34.clone.1), dimensions={0}, to_apply=%region_1.2 | reduce | flops 3670016 | bytes 18874372 | tf_op jit(solution)/shard_map/reduce_sum | solution.py:35
  252.3 0.0 copy-done
  252.3 0.0 copy-done.2
  252.3 1.9 multiply_convert_fusion
  254.2 12.4 %fusion.8 = f32[128,2048]{1,0:T(8,128)} fusion(bf16[128,4096]{1,0:T(8,128)(2,1)S(1)} %multiply_convert_fusion, bf16[2048,4096]{1,0:T(8,128)(2,1)} %param.8), kind=kOutput, calls=%fused_computation.22 | convolution fusion | flops 2147483648 | bytes 18874368 | tf_op jit(solution)/shard_map/dot_general | solution.py:43
  266.6 0.0 reduce-scatter.5.cloned.1.call-update
  266.6 0.1 dynamic-slice_multiply_fusion
  266.7 0.1 convert_reduce_fusion
  266.8 0.0 copy-start.1
  266.8 12.0 %fusion.2 = bf16[2048,4096]{1,0:T(8,128)(2,1)} fusion(bf16[2048,4096]{1,0:T(8,128)(2,1)} %param.8, f32[2048]{0:T(1024)S(1)} %multiply_divide_fusion, bf16[128,2048]{1,0:T(8,128)(2,1)S(1)} %all_gather.16, bf16[128,4096]{1,0:T(8,128)(2,1)S(1)} %multiply_convert_fusion), kind=kOutput, calls=%fused_computation.4 | convolution fusion | flops 2181038080 | bytes 35135488 | tf_op jit(solution)/shard_map/dot_general | solution.py:54
  278.8 14.1 %reduce-scatter.5.cloned.1.call-done = f32[128,512]{1,0:T(8,128)} async-done(((f32[128,2048]{1,0:T(8,128)}), f32[128,512]{1,0:T(8,128)}) %reduce-scatter.5.cloned.1.call-update) | async-done | bytes 262160 | tf_op jit(solution)/shard_map/reduce_scatter | solution.py:46
  292.9 0.0 copy-done.1
  292.9 1.0 multiply_convert_fusion.1
  293.9 10.1 %all_gather.19 = bf16[128,2048]{1,0:T(8,128)(2,1)S(1)} all-gather(bf16[128,512]{1,0:T(8,128)(2,1)S(1)} %multiply_convert_fusion.1), channel_id=1, replica_groups=mesh['layer'=4,'latent'=8] {'layer'}, dimensions={1}, use_global_device_ids=true | all-gather | bytes 655360 | tf_op jit(solution)/shard_map/all_gather | solution.py:49
  304.0 8.1 %convert_bitcast_fusion = bf16[4096,2048]{0,1:T(8,128)(2,1)} fusion(bf16[128,2048]{1,0:T(8,128)(2,1)S(1)} %all_gather.19, bf16[128,4096]{1,0:T(8,128)(2,1)S(1)} %copy-done), kind=kOutput, calls=%fused_computation.5 | convolution fusion | flops 2155872256 | bytes 18350080 | tf_op jit(solution)/shard_map/dot_general | solution.py:50
  312.1 22.4 %copy.8 = bf16[4096,2048]{1,0:T(8,128)(2,1)} copy(bf16[4096,2048]{0,1:T(8,128)(2,1)} %convert_bitcast_fusion) | data formatting | bytes 33554432
  (4 shorter events, 0.1 us)
Async XLA Ops:
  7.2 27.4 %all-gather.4.cloned.1.call-start = ((), (), s32[]{:S(2)}) async-start(), calls=%async_computation.2 | async-start | bytes 1179648 | tf_op jit(solution)/shard_map/all_gather | solution.py:26
  7.9 63.8 %reduce-scatter.3.cloned.1.call-start = ((), (), s32[]{:S(2)}) async-start(), calls=%async_computation.3 | async-start | bytes 1310720 | tf_op jit(solution)/shard_map/reduce_scatter | solution.py:30
  44.0 199.6 %all-gather.6.cloned.1.call-start = ((), (), s32[]{:S(2)}) async-start(), calls=%async_computation.5 | async-start | bytes 18874368 | tf_op jit(solution)/shard_map/all_gather | solution.py:36
  92.4 200.5 %reduce-scatter.5.cloned.1.call-start = ((), (), s32[]{:S(2)}) async-start(), calls=%async_computation.4 | async-start | bytes 1310720 | tf_op jit(solution)/shard_map/reduce_scatter | solution.py:46
  92.4 159.8 %copy-start = (bf16[128,4096]{1,0:T(8,128)(2,1)S(1)}, bf16[128,4096]{1,0:T(8,128)(2,1)}, u32[]{:S(2)}) copy-start(bf16[128,4096]{1,0:T(8,128)(2,1)} %all-gather.4.cloned.1.call-done) | copy-start | bytes 3145732
  92.4 159.8 %copy-start.2 = (f32[4096]{0:T(1024)S(1)}, f32[4096]{0:T(1024)}, u32[]{:S(2)}) copy-start(f32[4096]{0:T(1024)} %param.9) | copy-start | bytes 49156
  266.8 26.1 %copy-start.1 = (f32[128,512]{1,0:T(8,128)S(1)}, f32[128,512]{1,0:T(8,128)}, u32[]{:S(2)}) copy-start(f32[128,512]{1,0:T(8,128)} %reduce-scatter.3.cloned.1.call-done) | copy-start | bytes 786436
Sparse Core Ops, SparseCore 0:
  9.6 24.9 all-gather.3
  44.1 27.5 reduce-scatter.2
  92.5 151.0 all-gather.5
  266.7 26.0 reduce-scatter.4
